TPU v7x, 128 devices: a whole 4x4x4 slice. The times are simulated.
128 devices in a mesh: seq: 8 (over x, core), tp: 16 (over y, z).
Axes of the slice: x: 4, y: 4, z: 4, core: 2. Of those that a mesh axis runs over, the one named last changes fastest.
Arguments:
- vit_input: bfloat16 [8192, 1280], P(('seq', 'tp')), may hold values from -6 to 6
- image_lengths: int32 [8, 2], P('seq'), may hold values from 1 to 192, 256 in all within a row
- positions: int32 [2048], replicated, may hold values from 0 to 2047, each once
- vit_ln_gain: float32 [1280], replicated, may hold values from 0.25 to 1.75
- w_qkv: bfloat16 [1280, 3, 1280], P(None, None, 'tp'), may hold values from -0.15625 to 0.15625
- w_proj: bfloat16 [1280, 1280], P('tp'), may hold values from -0.15625 to 0.15625
- merger_ln_gain: float32 [1280], replicated, may hold values from 0.25 to 1.75
- merger_w1: bfloat16 [5120, 5120], P(None, 'tp'), may hold values from -0.078125 to 0.078125
- merger_w2: bfloat16 [5120, 8192], P('tp'), may hold values from -0.36336105 to 0.36336105
- norm_gain: float32 [8192], P('seq'), may hold values from 0.25 to 1.75
- gate_up_weight: bfloat16 [8192, 2, 29568], P('seq', None, 'tp'), may hold values from -0.0625 to 0.0625
- down_weight: bfloat16 [29568, 8192], P('tp', 'seq'), may hold values from -0.125 to 0.125
Outputs:
- mixed: bfloat16 [2048, 8192], P('tp', 'seq')
Inputs may be any that keep to these rules, and one draw needn't show every extreme that they name: `image_lengths`: each row sums to 256. `positions`: a permutation: every slot once.
All inputs are finite; a program needn't handle non-finite values.
Results may differ from a plain program's by a relative error of at most 0.038.
Values may be sent and summed in bfloat16 or wider, within the bound.
A program may use at most 128 MiB of HBM per device.

v0:
```python
import jax
import jax.numpy as jnp
from jax import lax
from jax.sharding import Mesh
from jax.sharding import PartitionSpec as P

D = 8192
HD = 80
TP = ("tp_0", "tp_1")
SEQ_TP = ("seq", "tp_0", "tp_1")


def from_everyone(x, axis):
    copies = jnp.broadcast_to(x, (lax.axis_size(axis), *x.shape))
    return lax.all_to_all(copies, axis, split_axis=0, concat_axis=0, tiled=True)


def laid_out(tiles, dim):
    shape = list(tiles.shape[1:])
    shape[dim] *= tiles.shape[0]
    return jnp.moveaxis(tiles, 0, dim).reshape(shape)


def gathered_copies(x, axis, dim):
    tiles = from_everyone(x, axis)
    return laid_out(tiles, dim)


def cut_along(x, dim, devices):
    before, after = (x.shape[:dim], x.shape[dim + 1 :])
    return jnp.moveaxis(x.reshape(*before, devices, -1, *after), dim, 0)


def sum_at_owner(x, axis, dim):
    devices = lax.axis_size(axis)
    tiles = lax.all_to_all(cut_along(x, dim, devices), axis, 0, 0, tiled=True)
    return jnp.sum(tiles.astype(jnp.float32), axis=0)


def over_copies(x, axis):
    everything = from_everyone(x, axis)
    return jnp.sum(everything, axis=0)


def sum_by_axis(x, axes, dim):
    if not axes:
        return x
    nearer = lax.psum_scatter(x, axes[0], scatter_dimension=dim, tiled=True)
    return sum_by_axis(nearer, axes[1:], dim)


def layer_norm(values, gain):
    mean = jnp.mean(values, axis=-1, keepdims=True)
    centered = values - mean
    variance = jnp.mean(centered * centered, axis=-1, keepdims=True)
    return centered * lax.rsqrt(variance + 1e-06) * gain


def image_ids(lengths, count):
    image_ends = jnp.cumsum(lengths) * 4
    patch_index = jnp.arange(count, dtype=jnp.int32)
    return jnp.sum((patch_index[:, None] >= image_ends[None, :]).astype(jnp.int32), axis=1)


def attend(query, keys, values, image_index):
    scores = jnp.einsum("qhe,khe->hqk", query, keys, preferred_element_type=jnp.float32) * HD ** (
        -0.5
    )
    same_image = image_index[:, None] == image_index[None, :]
    scores = jnp.where(same_image[None], scores, -1e30)
    top = jnp.max(scores, axis=-1, keepdims=True)
    expo = jnp.exp(scores - top)
    weights = (expo / jnp.sum(expo, axis=-1, keepdims=True)).astype(jnp.bfloat16)
    output = jnp.einsum("hqk,khe->qhe", weights, values, preferred_element_type=jnp.float32)
    return output.astype(jnp.bfloat16)


def slot_sources(positions):
    count = positions.shape[0]
    return jnp.zeros((count,), jnp.int32).at[positions].set(jnp.arange(count, dtype=jnp.int32))


def local(
    vit_input,
    image_lengths,
    positions,
    vit_ln_gain,
    w_qkv,
    w_proj,
    merger_ln_gain,
    merger_w1,
    merger_w2,
    norm_gain,
    gate_up_weight,
    down_weight,
):
    tp_size = lax.axis_size(TP)
    seq_size = lax.axis_size("seq")
    own_patches = vit_input.shape[0]
    patch_width = vit_input.shape[1]
    head_cols = w_qkv.shape[2]
    local_heads = head_cols // HD
    normed_patches = layer_norm(vit_input.astype(jnp.float32), vit_ln_gain).astype(jnp.bfloat16)
    w_qkv_flat = w_qkv.reshape(patch_width, 3 * head_cols)
    projected = jnp.dot(
        gathered_copies(normed_patches, TP, 0), w_qkv_flat, preferred_element_type=jnp.float32
    ).astype(jnp.bfloat16)
    group_patches = projected.shape[0]
    projected = projected.reshape(group_patches, 3, local_heads, HD)
    image_index = image_ids(image_lengths[0], group_patches)
    attended = attend(projected[:, 0], projected[:, 1], projected[:, 2], image_index).reshape(
        group_patches, head_cols
    )
    picked = attended
    attn_sum = sum_at_owner(
        jnp.dot(picked, w_proj, preferred_element_type=jnp.float32).astype(jnp.bfloat16), TP, 0
    )
    vit_out = vit_input.astype(jnp.float32) + attn_sum
    own_tokens = own_patches // 4
    merged_in = (
        layer_norm(vit_out, merger_ln_gain)
        .astype(jnp.bfloat16)
        .reshape(own_tokens, 4 * patch_width)
    )
    expanded = jax.nn.gelu(
        jnp.dot(gathered_copies(merged_in, TP, 0), merger_w1, preferred_element_type=jnp.float32),
        approximate=False,
    ).astype(jnp.bfloat16)
    picked = expanded
    vis_rows = sum_at_owner(
        jnp.dot(picked, merger_w2, preferred_element_type=jnp.float32).astype(jnp.bfloat16), TP, 0
    ).astype(jnp.bfloat16)
    blocks = lax.all_to_all(vis_rows, "seq", split_axis=1, concat_axis=0, tiled=True)
    gathered = lax.all_gather(blocks, TP, axis=0, tiled=True)
    col_width = gathered.shape[1]
    all_tokens = (
        gathered.reshape(tp_size, seq_size, own_tokens, col_width)
        .transpose(1, 0, 2, 3)
        .reshape(tp_size * seq_size * own_tokens, col_width)
    )
    seq_rows = all_tokens.shape[0]
    seq_tokens = jnp.take(all_tokens, slot_sources(positions), axis=0)
    token_values = seq_tokens.astype(jnp.float32)
    row_squares = over_copies(jnp.sum(token_values * token_values, axis=1), "seq")
    inverse_rms = lax.rsqrt(row_squares / D + 1e-06)
    normed = (token_values * inverse_rms[:, None] * norm_gain).astype(jnp.bfloat16)
    slice_width = seq_tokens.shape[1]
    hidden_width = gate_up_weight.shape[2]
    weight_flat = gate_up_weight.reshape(slice_width, 2 * hidden_width)
    out_rows = seq_rows // tp_size
    picked = normed
    gate_up = lax.psum_scatter(
        jnp.dot(picked, weight_flat, preferred_element_type=jnp.float32).astype(jnp.bfloat16),
        "seq",
        scatter_dimension=0,
        tiled=True,
    ).astype(jnp.float32)
    hidden = (jax.nn.silu(gate_up[:, :hidden_width]) * gate_up[:, hidden_width:]).astype(
        jnp.bfloat16
    )
    terms = jnp.dot(
        lax.all_gather(hidden, "seq", axis=0, tiled=True),
        down_weight,
        preferred_element_type=jnp.float32,
    )
    down_sum = sum_by_axis(terms.astype(jnp.bfloat16), TP, 0).astype(jnp.float32)
    residual = lax.dynamic_slice_in_dim(token_values, lax.axis_index(TP) * out_rows, out_rows, 0)
    return (residual + down_sum).astype(jnp.bfloat16)


def solution(mesh):
    finer = Mesh(mesh.devices.reshape(mesh.shape["seq"], 4, 4), ("seq", "tp_0", "tp_1"))
    in_specs = (
        P(SEQ_TP, None),
        P("seq", None),
        P(),
        P(),
        P(None, None, TP),
        P(TP, None),
        P(),
        P(None, TP),
        P(TP, None),
        P("seq"),
        P("seq", None, TP),
        P(TP, "seq"),
    )
    out_specs = P(TP, "seq")
    return jax.shard_map(local, mesh=finer, in_specs=in_specs, out_specs=out_specs, check_vma=False)
```

profile of v0, /device:TPU:0, one launch (start us, length us, event | category | flops | bytes accessed | tf_op | source)
XLA Modules:
  0.0 555.1 jit_solution(18318716780304703547)
XLA Ops:
  6.5 0.0 copy-start
  6.5 1.2 convert_reduce_fusion.1
  7.7 1.1 fusion.11
  8.9 0.0 copy-start.8
  8.9 1.0 fusion.13
  9.9 1.8 broadcast_in_dim.26
  11.7 8.2 %all-to-all-start = ((bf16[16,64,1280]{2,1,0:T(8,128)(2,1)}), bf16[16,64,1280]{2,1,0:T(8,128)(2,1)}, u32[]{:S(2)}, u32[]{:S(2)}) async-start(bf16[16,64,1280]{2,1,0:T(8,128)(2,1)} %broadcast_in_dim.26), calls=%async_computation | async-start | bytes 5242880 | tf_op jit(solution)/shard_map/all_to_all | solution.py:15
  19.9 0.0 all-gather.3.cloned.1.call-start
  20.0 0.0 copy-done.8
  20.0 0.2 reduce-window.8
  20.2 0.1 fusion.57
  20.3 36.8 %all-to-all-done = bf16[16,64,1280]{2,1,0:T(8,128)(2,1)} async-done(((bf16[16,64,1280]{2,1,0:T(8,128)(2,1)}), bf16[16,64,1280]{2,1,0:T(8,128)(2,1)}, u32[]{:S(2)}, u32[]{:S(2)}) %all-to-all-start) | async-done | bytes 2621472 | tf_op jit(solution)/shard_map/all_to_all | solution.py:15
  57.1 2.7 convolution_convert_fusion.4
  59.8 0.0 copy-start.9
  59.8 0.0 copy-start.6
  59.8 0.9 fusion.4
  60.7 0.0 copy-start.3
  60.7 0.0 copy-done.9
  60.7 1.9 copy-done.3
  62.6 1.0 fusion.3
  63.6 0.0 copy-done.6
  63.6 6.0 %convolution_convert_fusion.2 = bf16[1024,1280]{1,0:T(8,128)(2,1)} fusion(bf16[80,1280]{1,0:T(8,128)(2,1)S(1)} %copy-done.6, f32[1024,1024]{0,1:T(8,128)} %copy-done.3, f32[1024]{0:T(1024)S(1)} %fusion.3, f32[1024]{0:T(1024)S(1)} %get-tuple-element.5, s32[1024]{0:T(1024)S(1)} %fusion.57, bf16[1024,3,1,80]{0,3,1,2:T(8,128)(2,1)} %bitcast.64), kind=kOutput, calls=%fused_computation.14 | convolution fusion | flops 385171456 | bytes 7200768 | tf_op jit(solution)/shard_map/dot_general | solution.py:116
  69.6 37.0 %all_to_all.45 = bf16[16,64,1280]{2,1,0:T(8,128)(2,1)S(1)} all-to-all(bf16[16,64,1280]{2,1,0:T(8,128)(2,1)} %bitcast.55), channel_id=1, replica_groups=mesh['seq'=8,'tp_0'=4,'tp_1'=4] {'tp_0','tp_1'}, dimensions={0} | all-to-all | bytes 5242880 | tf_op jit(solution)/shard_map/all_to_all | solution.py:36
  106.6 0.4 convert_reduce_fusion
  107.0 0.0 copy-done.2
  107.0 0.1 fusion.56
  107.1 0.2 multiply_reduce_fusion.1
  107.4 0.0 copy-done.5
  107.4 0.1 multiply_convert_fusion.2
  107.5 0.8 reshape.148
  108.3 1.2 broadcast_in_dim.47
  109.5 35.3 %all_to_all.46 = bf16[16,16,5120]{2,1,0:T(8,128)(2,1)} all-to-all(bf16[16,16,5120]{2,1,0:T(8,128)(2,1)S(1)} %broadcast_in_dim.47), channel_id=1, replica_groups=mesh['seq'=8,'tp_0'=4,'tp_1'=4] {'tp_0','tp_1'}, dimensions={0} | all-to-all | bytes 5242880 | tf_op jit(solution)/shard_map/all_to_all | solution.py:15
  144.8 0.0 copy-done
  144.8 10.9 %convolution_convert_fusion.1 = bf16[256,8192]{1,0:T(8,128)(2,1)} fusion(bf16[320,8192]{1,0:T(8,128)(2,1)} %param.20, bf16[256,5120]{1,0:T(8,128)(2,1)} %bitcast.56, bf16[5120,320]{0,1:T(8,128)(2,1)S(1)} %copy-done), kind=kOutput, calls=%fused_computation.3 | convolution fusion | flops 2188460032 | bytes 15335424 | tf_op jit(solution)/shard_map/dot_general | solution.py:131
  155.7 51.6 %all_to_all.47 = bf16[16,16,8192]{2,1,0:T(8,128)(2,1)} all-to-all(bf16[16,16,8192]{2,1,0:T(8,128)(2,1)} %bitcast.54), channel_id=1, replica_groups=mesh['seq'=8,'tp_0'=4,'tp_1'=4] {'tp_0','tp_1'}, dimensions={0} | all-to-all | bytes 8388608 | tf_op jit(solution)/shard_map/all_to_all | solution.py:36
  207.3 2.9 reduce_sum.100
  210.2 11.7 %all_to_all.48 = bf16[16,8,1024]{2,0,1:T(8,128)(2,1)} all-to-all(bf16[16,8,1024]{2,0,1:T(8,128)(2,1)S(1)} %bitcast.59), channel_id=1, replica_groups=mesh['seq'=8,'tp_0'=4,'tp_1'=4] {'seq'}, dimensions={1} | all-to-all | bytes 524288 | tf_op jit(solution)/shard_map/all_to_all | solution.py:133
  221.9 0.0 all-gather.3.cloned.1.call-update
  222.0 0.0 reduce-scatter.4.cloned.1.call-start
  222.0 8.0 %scatter_custom_fusion = s32[2048]{0:T(1024)S(1)} fusion(s32[2048]{0:T(1024)S(1)} %compare_select_fusion.1, s32[2048]{0:T(1024)S(1)} %iota.7, s32[]{:T(128)} %constant.45.clone.1), kind=kCustom, calls=%fused_computation.97 | custom fusion | bytes 8196 | tf_op jit(solution)/shard_map/scatter | solution.py:80
  230.1 39.4 %all-gather.3.cloned.1.call-done = bf16[2048,1024]{1,0:T(8,128)(2,1)} async-done(((bf16[128,1024]{1,0:T(8,128)(2,1)}), bf16[2048,1024]{1,0:T(8,128)(2,1)}) %all-gather.3.cloned.1.call-update) | async-done | bytes 4194320 | tf_op jit(solution)/shard_map/all_gather | solution.py:134
  269.6 5.0 copy.21
  274.6 13.7 %gather_fusion = bf16[2048,1024]{1,0:T(8,128)(2,1)} fusion(bf16[2048,1024]{1,0:T(8,128)(2,1)} %bitcast.52, s32[2048]{0:T(1024)S(1)} %fusion.58), kind=kCustom, calls=%fused_computation | custom fusion | bytes 8396800 | tf_op jit(solution)/shard_map/jit(_take)/gather | solution.py:142
  288.2 3.1 multiply_reduce_fusion
  291.4 9.7 %all_to_all.49 = f32[8,1,2048]{2,1,0:T(1,128)S(1)} all-to-all(f32[8,1,2048]{2,1,0:T(1,128)S(1)} %broadcast_in_dim.50), channel_id=1, replica_groups=mesh['seq'=8,'tp_0'=4,'tp_1'=4] {'seq'}, dimensions={0} | all-to-all | bytes 131072 | tf_op jit(solution)/shard_map/all_to_all | solution.py:15
  301.1 0.1 reduce_sum.102
  301.1 22.3 %convolution_convert_fusion = bf16[2048,3696]{0,1:T(8,128)(2,1)} fusion(bf16[1024,3696]{0,1:T(8,128)(2,1)} %bitcast.60, f32[1024]{0:T(1024)S(1)} %copy-done.7, f32[2048]{0:T(1024)S(1)} %add_rsqrt_fusion, bf16[2048,1024]{1,0:T(8,128)(2,1)} %gather_fusion, pred[2048]{0:T(1024)(128)(4,1)S(1)} %compare_and_fusion), kind=kOutput, calls=%fused_computation.2 | convolution fusion | flops 15520202752 | bytes 26916864 | tf_op jit(solution)/shard_map/dot_general | solution.py:153
  323.5 0.0 reduce-scatter.4.cloned.1.call-update
  323.5 0.0 all-gather.5.cloned.1.call-start
  323.5 82.4 %reduce-scatter.4.cloned.1.call-done = bf16[256,3696]{0,1:T(8,128)(2,1)} async-done(((bf16[2048,3696]{0,1:T(8,128)(2,1)}), bf16[256,3696]{0,1:T(8,128)(2,1)}) %reduce-scatter.4.cloned.1.call-update) | async-done | bytes 1892368 | tf_op jit(solution)/shard_map/reduce_scatter | solution.py:152
  405.9 1.8 convert_element_type.83
  407.7 1.6 fusion.6
  409.3 0.0 all-gather.5.cloned.1.call-update
  409.3 0.0 reduce-scatter.6.cloned.1.call-start
  409.4 49.6 %all-gather.5.cloned.1.call-done = bf16[2048,1848]{0,1:T(8,128)(2,1)} async-done(((bf16[256,1848]{0,1:T(8,128)(2,1)}), bf16[2048,1848]{0,1:T(8,128)(2,1)}) %all-gather.5.cloned.1.call-update) | async-done | bytes 7569424 | tf_op jit(solution)/shard_map/all_gather | solution.py:162
  459.0 13.7 %convolution_convert_fusion.3 = bf16[2048,1024]{1,0:T(8,128)(2,1)} fusion(bf16[2048,1848]{0,1:T(8,128)(2,1)} %all-gather.5.cloned.1.call-done, bf16[1848,1024]{1,0:T(8,128)(2,1)} %param.23), kind=kOutput, calls=%fused_computation.15 | convolution fusion | flops 7753170944 | bytes 15548416 | tf_op jit(solution)/shard_map/dot_general | solution.py:161
  472.7 0.0 reduce-scatter.6.cloned.1.call-update
  472.7 0.0 reduce-scatter.8.cloned.1.call-start
  472.8 47.9 %reduce-scatter.6.cloned.1.call-done = bf16[512,1024]{1,0:T(8,128)(2,1)} async-done(((bf16[2048,1024]{1,0:T(8,128)(2,1)}), bf16[512,1024]{1,0:T(8,128)(2,1)}) %reduce-scatter.6.cloned.1.call-update) | async-done | bytes 1048592 | tf_op jit(solution)/shard_map/reduce_scatter | solution.py:48
  520.7 0.0 reduce-scatter.8.cloned.1.call-update
  520.7 0.0 copy-start.1
  520.8 5.3 fusion.95
  526.1 20.6 %reduce-scatter.8.cloned.1.call-done = bf16[128,1024]{1,0:T(8,128)(2,1)} async-done(((bf16[512,1024]{1,0:T(8,128)(2,1)}), bf16[128,1024]{1,0:T(8,128)(2,1)}) %reduce-scatter.8.cloned.1.call-update) | async-done | bytes 262160 | tf_op jit(solution)/shard_map/reduce_scatter | solution.py:48
  546.7 1.9 add_convert_fusion
  (19 shorter events, 0.1 us)
Async XLA Ops:
  6.5 138.2 %copy-start = (bf16[5120,320]{0,1:T(8,128)(2,1)S(1)}, bf16[5120,320]{0,1:T(8,128)(2,1)}, u32[]{:S(2)}) copy-start(bf16[5120,320]{0,1:T(8,128)(2,1)} %param.19) | copy-start | bytes 9830404
  8.9 11.1 %copy-start.8 = (s32[1,2]{1,0:T(1,128)S(1)}, s32[1,2]{1,0:T(1,128)}, u32[]{:S(2)}) copy-start(s32[1,2]{1,0:T(1,128)} %param.13) | copy-start | bytes 28
  11.7 45.3 %all-to-all-start = ((bf16[16,64,1280]{2,1,0:T(8,128)(2,1)}), bf16[16,64,1280]{2,1,0:T(8,128)(2,1)}, u32[]{:S(2)}, u32[]{:S(2)}) async-start(bf16[16,64,1280]{2,1,0:T(8,128)(2,1)} %broadcast_in_dim.26), calls=%async_computation | async-start | bytes 5242880 | tf_op jit(solution)/shard_map/all_to_all | solution.py:15
  19.9 249.6 %all-gather.3.cloned.1.call-start = ((), (), s32[]{:S(2)}) async-start(), calls=%async_computation.9 | async-start | bytes 4456448 | tf_op jit(solution)/shard_map/all_gather | solution.py:134
  59.8 0.9 copy-start.9
  59.8 3.8 copy-start.6
  60.7 1.9 copy-start.3
  69.6 37.4 %copy-start.2 = (bf16[64,1280]{1,0:T(8,128)(2,1)S(1)}, bf16[64,1280]{1,0:T(8,128)(2,1)}, u32[]{:S(2)}) copy-start(bf16[64,1280]{1,0:T(8,128)(2,1)} %param.12) | copy-start | bytes 491524
  69.6 37.7 %copy-start.5 = (f32[1280]{0:T(1024)S(1)}, f32[1280]{0:T(1024)}, u32[]{:S(2)}) copy-start(f32[1280]{0:T(1024)} %param.18) | copy-start | bytes 15364
  207.3 14.7 %copy-start.4 = (s32[2048]{0:T(1024)S(1)}, s32[2048]{0:T(1024)}, u32[]{:S(2)}) copy-start(s32[2048]{0:T(1024)} %param.14) | copy-start | bytes 24580
  222.0 184.0 %reduce-scatter.4.cloned.1.call-start = ((), (), s32[]{:S(2)}) async-start(), calls=%async_computation.10 | async-start | bytes 17031168 | tf_op jit(solution)/shard_map/reduce_scatter | solution.py:152
  288.2 12.9 %copy-start.7 = (f32[1024]{0:T(1024)S(1)}, f32[1024]{0:T(1024)}, u32[]{:S(2)}) copy-start(f32[1024]{0:T(1024)} %param.21) | copy-start | bytes 12292
  323.5 135.5 %all-gather.5.cloned.1.call-start = ((), (), s32[]{:S(2)}) async-start(), calls=%async_computation.11 | async-start | bytes 8515584 | tf_op jit(solution)/shard_map/all_gather | solution.py:162
  409.3 111.4 %reduce-scatter.6.cloned.1.call-start = ((), (), s32[]{:S(2)}) async-start(), calls=%async_computation.12 | async-start | bytes 5242880 | tf_op jit(solution)/shard_map/reduce_scatter | solution.py:48
  472.7 74.0 %reduce-scatter.8.cloned.1.call-start = ((), (), s32[]{:S(2)}) async-start(), calls=%async_computation.13 | async-start | bytes 1310720 | tf_op jit(solution)/shard_map/reduce_scatter | solution.py:48
  520.7 27.8 %copy-start.1 = (bf16[5120,320]{0,1:T(8,128)(2,1)S(1)}, bf16[5120,320]{0,1:T(8,128)(2,1)}, u32[]{:S(2)}) copy-start(bf16[5120,320]{0,1:T(8,128)(2,1)} %param.19) | copy-start | bytes 9830404
Sparse Core Ops, SparseCore 0:
  222.1 47.4 all-gather.2
  323.6 82.2 reduce-scatter.3
  409.4 49.4 all-gather.4
  472.9 47.8 reduce-scatter.5
  523.0 23.6 reduce-scatter.7
where the time goes:
time: 556 us; the launch traced here: 555 us
  waiting for transfers between devices  277 us (50%)
  blocking collectives  145 us (26%)
  matrix products  56.6 us (10%)
  local copies, waits for them, and re-layouts  32.5 us (6%)
  other arithmetic  22.1 us (4%)
  between operations  13.4 us (2%)
  starting transfers between devices  8.41 us (2%)
    all_to_all x2, blocking collectives, sum_at_owner(): tiles = lax.all_to_all(cut_along(x, dim, devices), axis, 0, 0, tiled=True)  88.6 us
    reduce_scatter x1, waiting for transfers between devices, local(): lax.psum_scatter(jnp.dot(picked, weight_flat, preferred_element_type=jnp....  82.4 us
    reduce_scatter x2, waiting for transfers between devices, sum_by_axis(): nearer = lax.psum_scatter(x, axes[0], scatter_dimension=dim, tiled=True)  68.6 us
    all_gather x1, waiting for transfers between devices, local(): lax.all_gather(hidden, 'seq', axis=0, tiled=True)  49.6 us
    all_to_all x2, blocking collectives, from_everyone(): return lax.all_to_all(copies, axis, split_axis=0, concat_axis=0, tiled=True)  45 us
    all_gather x1, waiting for transfers between devices, local(): gathered = lax.all_gather(blocks, TP, axis=0, tiled=True)  39.4 us
    all_to_all x1, waiting for transfers between devices, from_everyone(): return lax.all_to_all(copies, axis, split_axis=0, concat_axis=0, tiled=True)  36.8 us
    dot_general x1, matrix products, local(): jnp.dot(picked, weight_flat, preferred_element_type=jnp.float32)  22.3 us
  transfers between devices with their start and end apart: 6, of which 6 were waited for; matrix products, arithmetic and copies ran while one was open for 2% of the time, Pallas kernels for 0%

commit v1 on v0

--- a/solution.py
+++ b/solution.py
@@ -8,6 +8,27 @@
 HD = 80
 TP = ("tp_0", "tp_1")
 SEQ_TP = ("seq", "tp_0", "tp_1")
+
+
+def collect(x, axis, dim):
+    devices, index, rows = (lax.axis_size(axis), lax.axis_index(axis), x.shape[dim])
+    right = [(i, (i + 1) % devices) for i in range(devices)]
+    downward = [(i, (i - 1) % devices) for i in range(devices)]
+    out = jnp.zeros((*x.shape[:dim], devices * rows, *x.shape[dim + 1 :]), x.dtype)
+    out = lax.dynamic_update_slice_in_dim(out, x, index * rows, axis=dim)
+    from_left = from_right = x
+    middle = devices // 2
+    for hop in range(1, middle + 1):
+        from_left = lax.ppermute(from_left, axis, right)
+        out = lax.dynamic_update_slice_in_dim(
+            out, from_left, (index - hop) % devices * rows, axis=dim
+        )
+        if hop < devices - middle:
+            from_right = lax.ppermute(from_right, axis, downward)
+            out = lax.dynamic_update_slice_in_dim(
+                out, from_right, (index + hop) % devices * rows, axis=dim
+            )
+    return out
 
 
 def from_everyone(x, axis):
@@ -158,11 +179,7 @@
     hidden = (jax.nn.silu(gate_up[:, :hidden_width]) * gate_up[:, hidden_width:]).astype(
         jnp.bfloat16
     )
-    terms = jnp.dot(
-        lax.all_gather(hidden, "seq", axis=0, tiled=True),
-        down_weight,
-        preferred_element_type=jnp.float32,
-    )
+    terms = jnp.dot(collect(hidden, "seq", 0), down_weight, preferred_element_type=jnp.float32)
     down_sum = sum_by_axis(terms.astype(jnp.bfloat16), TP, 0).astype(jnp.float32)
     residual = lax.dynamic_slice_in_dim(token_values, lax.axis_index(TP) * out_rows, out_rows, 0)
     return (residual + down_sum).astype(jnp.bfloat16)

time: 556 us -> 565 us (1.016)
  local copies, waits for them, and re-layouts: 32.5 us -> 46.4 us
  waiting for transfers between devices: 277 us -> 265 us
  starting transfers between devices: 8.41 us -> 17.4 us
    all_gather x1 -> x0, waiting for transfers between devices: 49.6 us -> none  [local(): lax.all_gather(hidden, 'seq', axis=0, tiled=True)]
    ppermute x0 -> x7, waiting for transfers between devices: none -> 39.5 us  [the longest x4 39.5 us: collect(): from_left = lax.ppermute(from_left, axis, right)]
    dynamic_update_slice x0 -> x7, local copies, waits for them, and re-layouts: none -> 9.91 us  [the longest x4 5.47 us: collect(): lax.dynamic_update_slice_in_dim(out, from_left, (index - hop) % devices *...]
    ppermute x0 -> x7, starting transfers between devices: none -> 9.03 us  [the longest x3 9.02 us: collect(): from_right = lax.ppermute(from_right, axis, downward)]
  transfers between devices with their start and end apart: 6 -> 12, of which waited for: 6 -> 9; matrix products, arithmetic and copies ran while one was open for 2% -> 4% of each run, Pallas kernels for 0% -> 0%
where the time goes in v1:
time: 565 us; the launch traced here: 564 us
  waiting for transfers between devices  265 us (47%)
  blocking collectives  145 us (26%)
  matrix products  55.6 us (10%)
  local copies, waits for them, and re-layouts  46.4 us (8%)
  other arithmetic  21.2 us (4%)
  starting transfers between devices  17.4 us (3%)
  between operations  13.5 us (2%)
    all_to_all x2, blocking collectives, sum_at_owner(): tiles = lax.all_to_all(cut_along(x, dim, devices), axis, 0, 0, tiled=True)  88.6 us
    reduce_scatter x1, waiting for transfers between devices, local(): lax.psum_scatter(jnp.dot(picked, weight_flat, preferred_element_type=jnp....  82.4 us
    reduce_scatter x2, waiting for transfers between devices, sum_by_axis(): nearer = lax.psum_scatter(x, axes[0], scatter_dimension=dim, tiled=True)  66.5 us
    all_to_all x2, blocking collectives, from_everyone(): return lax.all_to_all(copies, axis, split_axis=0, concat_axis=0, tiled=True)  45 us
    ppermute x4, waiting for transfers between devices, collect(): from_left = lax.ppermute(from_left, axis, right)  39.5 us
    all_gather x1, waiting for transfers between devices, local(): gathered = lax.all_gather(blocks, TP, axis=0, tiled=True)  39.4 us
    all_to_all x1, waiting for transfers between devices, from_everyone(): return lax.all_to_all(copies, axis, split_axis=0, concat_axis=0, tiled=True)  36.8 us
    dot_general x1, matrix products, local(): jnp.dot(picked, weight_flat, preferred_element_type=jnp.float32)  22.3 us
  transfers between devices with their start and end apart: 12, of which 9 were waited for; matrix products, arithmetic and copies ran while one was open for 4% of the time, Pallas kernels for 0%

profile of v1, /device:TPU:0, one launch (start us, length us, event | category | flops | bytes accessed | tf_op | source)
XLA Modules:
  0.0 563.9 jit_solution(9632567118443035827)
XLA Ops:
  6.5 1.2 convert_reduce_fusion.1
  7.7 1.1 fusion.11
  8.9 1.0 fusion.13
  9.9 1.8 broadcast_in_dim.48
  11.7 8.2 %all-to-all-start = ((bf16[16,64,1280]{2,1,0:T(8,128)(2,1)}), bf16[16,64,1280]{2,1,0:T(8,128)(2,1)}, u32[]{:S(2)}, u32[]{:S(2)}) async-start(bf16[16,64,1280]{2,1,0:T(8,128)(2,1)} %broadcast_in_dim.48), calls=%async_computation | async-start | bytes 5242880 | tf_op jit(solution)/shard_map/all_to_all | solution.py:36
  19.9 0.0 all-gather.2.cloned.1.call-start
  20.0 0.2 reduce-window.8
  20.2 0.1 fusion.57
  20.3 36.8 %all-to-all-done = bf16[16,64,1280]{2,1,0:T(8,128)(2,1)} async-done(((bf16[16,64,1280]{2,1,0:T(8,128)(2,1)}), bf16[16,64,1280]{2,1,0:T(8,128)(2,1)}, u32[]{:S(2)}, u32[]{:S(2)}) %all-to-all-start) | async-done | bytes 2621472 | tf_op jit(solution)/shard_map/all_to_all | solution.py:36
  57.1 2.7 convolution_convert_fusion.4
  59.8 0.9 fusion.4
  60.7 1.9 copy-done.4
  62.6 1.0 fusion.3
  63.6 6.0 %convolution_convert_fusion.2 = bf16[1024,1280]{1,0:T(8,128)(2,1)} fusion(bf16[80,1280]{1,0:T(8,128)(2,1)S(1)} %copy-done.9, f32[1024,1024]{0,1:T(8,128)} %copy-done.4, f32[1024]{0:T(1024)S(1)} %fusion.3, f32[1024]{0:T(1024)S(1)} %get-tuple-element.7, s32[1024]{0:T(1024)S(1)} %fusion.57, bf16[1024,3,1,80]{0,3,1,2:T(8,128)(2,1)} %bitcast.64), kind=kOutput, calls=%fused_computation.14 | convolution fusion | flops 385171456 | bytes 7200768 | tf_op jit(solution)/shard_map/dot_general | solution.py:137
  69.6 37.0 %all_to_all.45 = bf16[16,64,1280]{2,1,0:T(8,128)(2,1)S(1)} all-to-all(bf16[16,64,1280]{2,1,0:T(8,128)(2,1)} %bitcast.55), channel_id=1, replica_groups=mesh['seq'=8,'tp_0'=4,'tp_1'=4] {'tp_0','tp_1'}, dimensions={0} | all-to-all | bytes 5242880 | tf_op jit(solution)/shard_map/all_to_all | solution.py:57
  106.6 0.4 convert_reduce_fusion
  107.0 0.1 fusion.56
  107.1 0.2 multiply_reduce_fusion.1
  107.4 0.1 multiply_convert_fusion.2
  107.5 0.8 reshape.148
  108.3 1.2 broadcast_in_dim.50
  109.5 35.3 %all_to_all.46 = bf16[16,16,5120]{2,1,0:T(8,128)(2,1)} all-to-all(bf16[16,16,5120]{2,1,0:T(8,128)(2,1)S(1)} %broadcast_in_dim.50), channel_id=1, replica_groups=mesh['seq'=8,'tp_0'=4,'tp_1'=4] {'tp_0','tp_1'}, dimensions={0} | all-to-all | bytes 5242880 | tf_op jit(solution)/shard_map/all_to_all | solution.py:36
  144.8 10.9 %convolution_convert_fusion.1 = bf16[256,8192]{1,0:T(8,128)(2,1)} fusion(bf16[320,8192]{1,0:T(8,128)(2,1)} %param.20, bf16[256,5120]{1,0:T(8,128)(2,1)} %bitcast.56, bf16[5120,320]{0,1:T(8,128)(2,1)S(1)} %copy-done), kind=kOutput, calls=%fused_computation.3 | convolution fusion | flops 2188460032 | bytes 15335424 | tf_op jit(solution)/shard_map/dot_general | solution.py:152
  155.7 51.6 %all_to_all.47 = bf16[16,16,8192]{2,1,0:T(8,128)(2,1)} all-to-all(bf16[16,16,8192]{2,1,0:T(8,128)(2,1)} %bitcast.54), channel_id=1, replica_groups=mesh['seq'=8,'tp_0'=4,'tp_1'=4] {'tp_0','tp_1'}, dimensions={0} | all-to-all | bytes 8388608 | tf_op jit(solution)/shard_map/all_to_all | solution.py:57
  207.3 2.9 reduce_sum.100
  210.2 11.7 %all_to_all.48 = bf16[16,8,1024]{2,0,1:T(8,128)(2,1)} all-to-all(bf16[16,8,1024]{2,0,1:T(8,128)(2,1)S(1)} %bitcast.59), channel_id=1, replica_groups=mesh['seq'=8,'tp_0'=4,'tp_1'=4] {'seq'}, dimensions={1} | all-to-all | bytes 524288 | tf_op jit(solution)/shard_map/all_to_all | solution.py:154
  221.9 0.0 all-gather.2.cloned.1.call-update
  222.0 0.0 reduce-scatter.4.cloned.1.call-start
  222.0 8.0 %scatter_custom_fusion = s32[2048]{0:T(1024)S(1)} fusion(s32[2048]{0:T(1024)S(1)} %compare_select_fusion.1, s32[2048]{0:T(1024)S(1)} %iota.7, s32[]{:T(128)} %constant.57.clone.1), kind=kCustom, calls=%fused_computation.97 | custom fusion | bytes 8196 | tf_op jit(solution)/shard_map/scatter | solution.py:101
  230.1 39.4 %all-gather.2.cloned.1.call-done = bf16[2048,1024]{1,0:T(8,128)(2,1)} async-done(((bf16[128,1024]{1,0:T(8,128)(2,1)}), bf16[2048,1024]{1,0:T(8,128)(2,1)}) %all-gather.2.cloned.1.call-update) | async-done | bytes 4194320 | tf_op jit(solution)/shard_map/all_gather | solution.py:155
  269.6 5.0 copy.21
  274.6 13.7 %gather_fusion = bf16[2048,1024]{1,0:T(8,128)(2,1)} fusion(bf16[2048,1024]{1,0:T(8,128)(2,1)} %bitcast.52, s32[2048]{0:T(1024)S(1)} %fusion.58), kind=kCustom, calls=%fused_computation | custom fusion | bytes 8396800 | tf_op jit(solution)/shard_map/jit(_take)/gather | solution.py:163
  288.2 3.1 multiply_reduce_fusion
  291.4 9.7 %all_to_all.49 = f32[8,1,2048]{2,1,0:T(1,128)S(1)} all-to-all(f32[8,1,2048]{2,1,0:T(1,128)S(1)} %broadcast_in_dim.54), channel_id=1, replica_groups=mesh['seq'=8,'tp_0'=4,'tp_1'=4] {'seq'}, dimensions={0} | all-to-all | bytes 131072 | tf_op jit(solution)/shard_map/all_to_all | solution.py:36
  301.1 0.1 reduce_sum.102
  301.1 22.3 %convolution_convert_fusion = bf16[2048,3696]{0,1:T(8,128)(2,1)} fusion(bf16[1024,3696]{0,1:T(8,128)(2,1)} %bitcast.60, f32[1024]{0:T(1024)S(1)} %copy-done.10, f32[2048]{0:T(1024)S(1)} %add_rsqrt_fusion, bf16[2048,1024]{1,0:T(8,128)(2,1)} %gather_fusion, pred[2048]{0:T(1024)(128)(4,1)S(1)} %compare_and_fusion), kind=kOutput, calls=%fused_computation.2 | convolution fusion | flops 15520202752 | bytes 26916864 | tf_op jit(solution)/shard_map/dot_general | solution.py:174
  323.5 0.0 reduce-scatter.4.cloned.1.call-update
  323.5 0.0 reduce-scatter.6.cloned.1.call-start
  323.5 82.4 %reduce-scatter.4.cloned.1.call-done = bf16[256,3696]{0,1:T(8,128)(2,1)} async-done(((bf16[2048,3696]{0,1:T(8,128)(2,1)}), bf16[256,3696]{0,1:T(8,128)(2,1)}) %reduce-scatter.4.cloned.1.call-update) | async-done | bytes 1892368 | tf_op jit(solution)/shard_map/reduce_scatter | solution.py:173
  405.9 1.8 convert_element_type.83
  407.7 0.9 broadcast_in_dim.53
  408.7 0.6 constant_dynamic-update-slice_fusion.7
  409.3 3.0 copy-done.2
  412.3 3.0 collective-permute-start.1
  415.3 11.4 %collective-permute-done = bf16[256,1848]{0,1:T(8,128)(2,1)S(1)} collective-permute-done((bf16[256,1848]{0,1:T(8,128)(2,1)S(1)}, bf16[256,1848]{0,1:T(8,128)(2,1)S(1)}, u32[]{:S(2)}, u32[]{:S(2)}) %collective-permute-start) | collective-permute-done | bytes 946208 | tf_op jit(solution)/shard_map/ppermute | solution.py:22
  426.7 3.1 collective-permute-start.3
  429.7 11.3 %collective-permute-done.2 = bf16[256,1848]{0,1:T(8,128)(2,1)S(1)} collective-permute-done((bf16[256,1848]{0,1:T(8,128)(2,1)S(1)}, bf16[256,1848]{0,1:T(8,128)(2,1)S(1)}, u32[]{:S(2)}, u32[]{:S(2)}) %collective-permute-start.2) | collective-permute-done | bytes 946208 | tf_op jit(solution)/shard_map/ppermute | solution.py:22
  441.0 2.2 constant_dynamic-update-slice_fusion.6
  443.3 3.0 collective-permute-start.5
  446.3 2.3 constant_dynamic-update-slice_fusion.5
  448.5 6.8 %collective-permute-done.4 = bf16[256,1848]{0,1:T(8,128)(2,1)S(1)} collective-permute-done((bf16[256,1848]{0,1:T(8,128)(2,1)S(1)}, bf16[256,1848]{0,1:T(8,128)(2,1)S(1)}, u32[]{:S(2)}, u32[]{:S(2)}) %collective-permute-start.4) | collective-permute-done | bytes 946208 | tf_op jit(solution)/shard_map/ppermute | solution.py:22
  455.4 1.1 constant_dynamic-update-slice_fusion.4
  456.5 1.1 constant_dynamic-update-slice_fusion.3
  457.5 1.1 constant_dynamic-update-slice_fusion.2
  458.6 1.1 constant_dynamic-update-slice_fusion.1
  459.7 10.0 %collective-permute-done.6 = bf16[256,1848]{0,1:T(8,128)(2,1)S(1)} collective-permute-done((bf16[256,1848]{0,1:T(8,128)(2,1)S(1)}, bf16[256,1848]{0,1:T(8,128)(2,1)S(1)}, u32[]{:S(2)}, u32[]{:S(2)}) %collective-permute-start.6) | collective-permute-done | bytes 946208 | tf_op jit(solution)/shard_map/ppermute | solution.py:22
  469.7 1.1 constant_dynamic-update-slice_fusion
  470.8 12.8 %convolution_convert_fusion.3 = bf16[2048,1024]{1,0:T(8,128)(2,1)} fusion(bf16[2048,1848]{0,1:T(8,128)(2,1)} %constant_dynamic-update-slice_fusion, bf16[1848,1024]{1,0:T(8,128)(2,1)S(1)} %copy-done.8), kind=kOutput, calls=%fused_computation.15 | convolution fusion | flops 7753170944 | bytes 15548416 | tf_op jit(solution)/shard_map/dot_general | solution.py:182
  483.6 0.0 reduce-scatter.6.cloned.1.call-update
  483.6 0.0 reduce-scatter.8.cloned.1.call-start
  483.7 45.8 %reduce-scatter.6.cloned.1.call-done = bf16[512,1024]{1,0:T(8,128)(2,1)} async-done(((bf16[2048,1024]{1,0:T(8,128)(2,1)}), bf16[512,1024]{1,0:T(8,128)(2,1)}) %reduce-scatter.6.cloned.1.call-update) | async-done | bytes 1048592 | tf_op jit(solution)/shard_map/reduce_scatter | solution.py:69
  529.5 5.3 fusion.95
  534.8 20.6 %reduce-scatter.8.cloned.1.call-done = bf16[128,1024]{1,0:T(8,128)(2,1)} async-done(((bf16[512,1024]{1,0:T(8,128)(2,1)}), bf16[128,1024]{1,0:T(8,128)(2,1)}) %reduce-scatter.8.cloned.1.call-update) | async-done | bytes 262160 | tf_op jit(solution)/shard_map/reduce_scatter | solution.py:69
  555.5 1.9 add_convert_fusion
  (44 shorter events, 0.2 us)
Async XLA Ops:
  6.5 138.2 %copy-start = (bf16[5120,320]{0,1:T(8,128)(2,1)S(1)}, bf16[5120,320]{0,1:T(8,128)(2,1)}, u32[]{:S(2)}) copy-start(bf16[5120,320]{0,1:T(8,128)(2,1)} %param.19) | copy-start | bytes 9830404
  8.9 11.1 %copy-start.11 = (s32[1,2]{1,0:T(1,128)S(1)}, s32[1,2]{1,0:T(1,128)}, u32[]{:S(2)}) copy-start(s32[1,2]{1,0:T(1,128)} %param.13) | copy-start | bytes 28
  11.7 45.3 %all-to-all-start = ((bf16[16,64,1280]{2,1,0:T(8,128)(2,1)}), bf16[16,64,1280]{2,1,0:T(8,128)(2,1)}, u32[]{:S(2)}, u32[]{:S(2)}) async-start(bf16[16,64,1280]{2,1,0:T(8,128)(2,1)} %broadcast_in_dim.48), calls=%async_computation | async-start | bytes 5242880 | tf_op jit(solution)/shard_map/all_to_all | solution.py:36
  19.9 249.6 %all-gather.2.cloned.1.call-start = ((), (), s32[]{:S(2)}) async-start(), calls=%async_computation.9 | async-start | bytes 4456448 | tf_op jit(solution)/shard_map/all_gather | solution.py:155
  59.8 0.9 copy-start.12
  59.8 3.8 copy-start.9
  60.7 1.9 copy-start.4
  69.6 37.4 %copy-start.3 = (bf16[64,1280]{1,0:T(8,128)(2,1)S(1)}, bf16[64,1280]{1,0:T(8,128)(2,1)}, u32[]{:S(2)}) copy-start(bf16[64,1280]{1,0:T(8,128)(2,1)} %param.12) | copy-start | bytes 491524
  69.6 37.7 %copy-start.7 = (f32[1280]{0:T(1024)S(1)}, f32[1280]{0:T(1024)}, u32[]{:S(2)}) copy-start(f32[1280]{0:T(1024)} %param.18) | copy-start | bytes 15364
  207.3 14.7 %copy-start.6 = (s32[2048]{0:T(1024)S(1)}, s32[2048]{0:T(1024)}, u32[]{:S(2)}) copy-start(s32[2048]{0:T(1024)} %param.14) | copy-start | bytes 24580
  222.0 184.0 %reduce-scatter.4.cloned.1.call-start = ((), (), s32[]{:S(2)}) async-start(), calls=%async_computation.10 | async-start | bytes 17031168 | tf_op jit(solution)/shard_map/reduce_scatter | solution.py:173
  288.2 12.9 %copy-start.10 = (f32[1024]{0:T(1024)S(1)}, f32[1024]{0:T(1024)}, u32[]{:S(2)}) copy-start(f32[1024]{0:T(1024)} %param.21) | copy-start | bytes 12292
  323.5 206.0 %reduce-scatter.6.cloned.1.call-start = ((), (), s32[]{:S(2)}) async-start(), calls=%async_computation.11 | async-start | bytes 5242880 | tf_op jit(solution)/shard_map/reduce_scatter | solution.py:69
  409.3 3.0 copy-start.2
  412.3 14.3 %collective-permute-start = (bf16[256,1848]{0,1:T(8,128)(2,1)S(1)}, bf16[256,1848]{0,1:T(8,128)(2,1)S(1)}, u32[]{:S(2)}, u32[]{:S(2)}) collective-permute-start(bf16[256,1848]{0,1:T(8,128)(2,1)S(1)} %get-tuple-element.6), channel_id=1, source_target_pairs={{0,16},{16,32},{32,48},{48,64},{64,80},{80,96},{96,112},{112,0},{1... | collective-permute-start | bytes 2838536 | tf_op jit(solution)/shard_map/ppermute | solution.py:22
  412.3 14.3 %collective-permute-start.1 = (bf16[256,1848]{0,1:T(8,128)(2,1)S(1)}, bf16[256,1848]{0,1:T(8,128)(2,1)}, u32[]{:S(2)}, u32[]{:S(2)}) collective-permute-start(bf16[256,1848]{0,1:T(8,128)(2,1)S(1)} %get-tuple-element.6), channel_id=1, source_target_pairs={{0,112},{16,0},{32,16},{48,32},{64,48},{80,64},{96,80},{112,96},{1... | collective-permute-start | bytes 2838536 | tf_op jit(solution)/shard_map/ppermute | solution.py:27
  426.7 14.3 %copy-start.5 = (bf16[256,1848]{0,1:T(8,128)(2,1)}, bf16[256,1848]{0,1:T(8,128)(2,1)S(1)}, u32[]{:S(2)}) copy-start(bf16[256,1848]{0,1:T(8,128)(2,1)S(1)} %collective-permute-done) | copy-start | bytes 2838532
  426.7 14.3 %collective-permute-start.2 = (bf16[256,1848]{0,1:T(8,128)(2,1)S(1)}, bf16[256,1848]{0,1:T(8,128)(2,1)S(1)}, u32[]{:S(2)}, u32[]{:S(2)}) collective-permute-start(bf16[256,1848]{0,1:T(8,128)(2,1)S(1)} %collective-permute-done), channel_id=1, source_target_pairs={{0,16},{16,32},{32,48},{48,64},{64,80},{80,96},{96,112},{112,0},{1... | collective-permute-start | bytes 2838536 | tf_op jit(solution)/shard_map/ppermute | solution.py:22
  426.7 16.6 %collective-permute-start.3 = (bf16[256,1848]{0,1:T(8,128)(2,1)}, bf16[256,1848]{0,1:T(8,128)(2,1)S(1)}, u32[]{:S(2)}, u32[]{:S(2)}) collective-permute-start(bf16[256,1848]{0,1:T(8,128)(2,1)} %collective-permute-done.1), channel_id=1, source_target_pairs={{0,112},{16,0},{32,16},{48,32},{64,48},{80,64},{96,80},{112,96},{1... | collective-permute-start | bytes 2838536 | tf_op jit(solution)/shard_map/ppermute | solution.py:27
  441.0 14.3 %collective-permute-start.4 = (bf16[256,1848]{0,1:T(8,128)(2,1)S(1)}, bf16[256,1848]{0,1:T(8,128)(2,1)S(1)}, u32[]{:S(2)}, u32[]{:S(2)}) collective-permute-start(bf16[256,1848]{0,1:T(8,128)(2,1)S(1)} %collective-permute-done.2), channel_id=1, source_target_pairs={{0,16},{16,32},{32,48},{48,64},{64,80},{80,96},{96,112},{112,0},{1... | collective-permute-start | bytes 2838536 | tf_op jit(solution)/shard_map/ppermute | solution.py:22
  443.3 15.3 %collective-permute-start.5 = (bf16[256,1848]{0,1:T(8,128)(2,1)S(1)}, bf16[256,1848]{0,1:T(8,128)(2,1)S(1)}, u32[]{:S(2)}, u32[]{:S(2)}) collective-permute-start(bf16[256,1848]{0,1:T(8,128)(2,1)S(1)} %collective-permute-done.3), channel_id=1, source_target_pairs={{0,112},{16,0},{32,16},{48,32},{64,48},{80,64},{96,80},{112,96},{1... | collective-permute-start | bytes 2838536 | tf_op jit(solution)/shard_map/ppermute | solution.py:27
  455.3 14.3 %collective-permute-start.6 = (bf16[256,1848]{0,1:T(8,128)(2,1)S(1)}, bf16[256,1848]{0,1:T(8,128)(2,1)S(1)}, u32[]{:S(2)}, u32[]{:S(2)}) collective-permute-start(bf16[256,1848]{0,1:T(8,128)(2,1)S(1)} %collective-permute-done.4), channel_id=1, source_target_pairs={{0,16},{16,32},{32,48},{48,64},{64,80},{80,96},{96,112},{112,0},{1... | collective-permute-start | bytes 2838536 | tf_op jit(solution)/shard_map/ppermute | solution.py:22
  456.5 14.3 %copy-start.8 = (bf16[1848,1024]{1,0:T(8,128)(2,1)S(1)}, bf16[1848,1024]{1,0:T(8,128)(2,1)}, u32[]{:S(2)}) copy-start(bf16[1848,1024]{1,0:T(8,128)(2,1)} %param.23) | copy-start | bytes 11354116
  483.6 71.9 %reduce-scatter.8.cloned.1.call-start = ((), (), s32[]{:S(2)}) async-start(), calls=%async_computation.12 | async-start | bytes 1310720 | tf_op jit(solution)/shard_map/reduce_scatter | solution.py:69
  529.5 27.8 %copy-start.1 = (bf16[5120,320]{0,1:T(8,128)(2,1)S(1)}, bf16[5120,320]{0,1:T(8,128)(2,1)}, u32[]{:S(2)}) copy-start(bf16[5120,320]{0,1:T(8,128)(2,1)} %param.19) | copy-start | bytes 9830404
Sparse Core Ops, SparseCore 0:
  222.1 47.4 all-gather.1
  323.6 82.2 reduce-scatter.3
  483.7 45.7 reduce-scatter.5
  531.7 23.6 reduce-scatter.7
